TPU v7x, 512 devices: a whole 4x8x8 slice. The times are simulated.
512 devices in a mesh: owner: 64 (over y, x, core), rows: 8 (over z).
Axes of the slice: x: 4, y: 8, z: 8, core: 2. Of those that a mesh axis runs over, the one named last changes fastest.
Arguments:
- train_down: float32 [64, 1024, 2048], P('owner', None, 'rows'), may hold values from -0.1875 to 0.1875
- router_weight: float32 [2048, 64], P('rows', 'owner'), may hold values from -0.125 to 0.125
- router_gain: float32 [2048], P('rows'), may hold values from 0.25 to 1.75
Outputs:
- ready_down: bfloat16 [64, 2048, 1024], P('owner')
- serve_router: bfloat16 [2048, 64], replicated
All inputs are finite; a program needn't handle non-finite values.
Results may differ from a plain program's by a relative error of at most 0.001.
Values may be sent and summed in bfloat16 or wider, within the bound.
No kernel may reach another device: no remote copies, remote signals or barrier semaphores. Data moves between devices by JAX's collectives and lax.ppermute only.
A program may use at most 64 MiB of HBM per device.

v0:
```python
import jax
import jax.numpy as jnp
from jax import lax
from jax.sharding import PartitionSpec as P


def in_order(blocks, dim):
    blocks = jnp.moveaxis(blocks, 0, dim)
    dims = blocks.shape
    return blocks.reshape(*dims[:dim], dims[dim] * dims[dim + 1], *dims[dim + 2 :])


def from_everyone(array, axis):
    copies = jnp.broadcast_to(array, (lax.axis_size(axis), *array.shape))
    return lax.all_to_all(copies, axis, split_axis=0, concat_axis=0, tiled=True)


def gather_directly(array, axis, dim):
    return in_order(from_everyone(array, axis), dim)


def on_device(train_down, router_weight, router_gain):
    narrow_down = train_down.astype(jnp.bfloat16)
    ready_down = lax.all_gather(narrow_down, "rows", axis=2, tiled=True)
    ready_down = jnp.transpose(ready_down, (0, 2, 1))
    part_router = (router_weight * router_gain[:, None]).astype(jnp.bfloat16)
    row_router = lax.all_gather(part_router, "rows", axis=0, tiled=True)
    serve_router = gather_directly(row_router, "owner", 1)
    return (ready_down, serve_router)


def solution(mesh):
    in_specs = (P("owner", None, "rows"), P("rows", "owner"), P("rows"))
    out_specs = (P("owner", None, None), P())
    return jax.shard_map(
        on_device, mesh=mesh, in_specs=in_specs, out_specs=out_specs, check_vma=False
    )
```

profile of v0, /device:TPU:1, one launch (start us, length us, event | category | flops | bytes accessed | tf_op | source)
XLA Modules:
  0.0 85.6 jit_solution(9226915147789131716)
XLA Ops:
  7.2 0.0 all-gather.2.cloned.1.call-start
  7.2 2.2 %copy.7 = bf16[1,1024,256]{1,2,0:T(8,128)(2,1)} copy(f32[1,1024,256]{2,1,0:T(8,128)} %param.3) | data formatting | bytes 1572864 | tf_op args[0]
  9.4 0.0 all-gather.2.cloned.1.call-update
  9.5 0.7 multiply_convert_fusion
  10.2 19.4 %all_gather.9 = bf16[2048,1]{0,1:T(2,128)(2,1)S(1)} all-gather(bf16[256,1]{0,1:T(2,128)(2,1)S(1)} %multiply_convert_fusion), channel_id=1, replica_groups=mesh['owner'=64,'rows'=8] {'rows'}, dimensions={0}, use_global_device_ids=true | all-gather | bytes 4608 | tf_op jit(solution)/shard_map/all_gather | solution.py:27
  29.6 0.3 broadcast_bitcast_fusion
  29.9 0.5 broadcast.2
  30.4 2.2 %reduce.1 = bf16[64,2048]{1,0:T(8,128)(2,1)S(1)} reduce(bf16[64,1,2048]{2,1,0:T(2,128)(2,1)S(1)} %broadcast_bitcast_fusion, bf16[]{:T(256)} %broadcast.2), dimensions={1}, to_apply=%broadcast_bitcast_fusion.reduce_sub_computation | reduce | bytes 524290
  32.5 0.2 reshape.10
  32.7 27.4 %all_to_all.5 = bf16[64,2,1024]{2,1,0:T(2,128)(2,1)S(1)} all-to-all(bf16[64,2,1024]{2,1,0:T(2,128)(2,1)S(1)} %reshape.10), channel_id=1, replica_groups=mesh['owner'=64,'rows'=8] {'owner'}, dimensions={0} | all-to-all | bytes 524288 | tf_op jit(solution)/shard_map/all_to_all | solution.py:15
  60.2 0.2 reshape.11
  60.4 0.9 copy.10
  61.2 12.9 %all-gather.2.cloned.1.call-done = bf16[1,1024,2048]{1,2,0:T(8,128)(2,1)} async-done(((bf16[1,1024,256]{1,2,0:T(8,128)(2,1)}), bf16[1,1024,2048]{1,2,0:T(8,128)(2,1)}) %all-gather.2.cloned.1.call-update) | async-done | bytes 4194320 | tf_op jit(solution)/shard_map/all_gather | solution.py:24
  74.2 4.6 %copy.12 = bf16[1,2048,1024]{2,1,0:T(8,128)(2,1)} copy(bf16[1,2048,1024]{2,1,0:T(8,128)(2,1)} %bitcast.10) | data formatting | bytes 8388608
  (1 shorter events, 0.0 us)
Async XLA Ops:
  7.2 67.0 %all-gather.2.cloned.1.call-start = ((), (), s32[]{:S(2)}) async-start(), calls=%async_computation.1 | async-start | bytes 4718592 | tf_op jit(solution)/shard_map/all_gather | solution.py:24
Sparse Core Ops, SparseCore 0:
  10.6 63.4 all-gather.1
where the time goes:
time: 85.9 us; the launch traced here: 85.6 us
  blocking collectives  46.8 us (54%)
  between operations  14.1 us (16%)
  waiting for transfers between devices  12.9 us (15%)
  local copies, waits for them, and re-layouts  8.91 us (10%)
  other arithmetic  2.89 us (3%)
    all_to_all x1, blocking collectives, from_everyone(): return lax.all_to_all(copies, axis, split_axis=0, concat_axis=0, tiled=True)  27.4 us
    all_gather x1, blocking collectives, on_device(): row_router = lax.all_gather(part_router, 'rows', axis=0, tiled=True)  19.4 us
    all_gather x1, waiting for transfers between devices, on_device(): ready_down = lax.all_gather(narrow_down, 'rows', axis=2, tiled=True)  12.9 us
    unnamed x6, local copies, waits for them, and re-layouts  8.05 us
    unnamed x1, other arithmetic  2.15 us
  transfers between devices with their start and end apart: 1, of which 1 were waited for; matrix products, arithmetic and copies ran while one was open for 6% of the time, Pallas kernels for 0%

commit v1 on v0

--- a/solution.py
+++ b/solution.py
@@ -21,7 +21,10 @@
 
 def on_device(train_down, router_weight, router_gain):
     narrow_down = train_down.astype(jnp.bfloat16)
-    ready_down = lax.all_gather(narrow_down, "rows", axis=2, tiled=True)
+    devices = lax.axis_size("rows")
+    pieces = jnp.stack([narrow_down for _ in range(devices)])
+    pieces = lax.all_to_all(pieces, "rows", split_axis=0, concat_axis=0)
+    ready_down = jnp.concatenate(pieces, axis=2)
     ready_down = jnp.transpose(ready_down, (0, 2, 1))
     part_router = (router_weight * router_gain[:, None]).astype(jnp.bfloat16)
     row_router = lax.all_gather(part_router, "rows", axis=0, tiled=True)

time: 85.9 us -> 161 us (1.87)
  waiting for transfers between devices: 12.9 us -> 107 us
  blocking collectives: 46.8 us -> 19.4 us
  starting transfers between devices: 0.04 us -> 19.1 us
  between operations: 14.1 us -> 0.68 us
    all_to_all x0 -> x2, waiting for transfers between devices: none -> 107 us  [the longest x1 95.7 us: on_device(): pieces = lax.all_to_all(pieces, 'rows', split_axis=0, concat_axis=0)]
    all_to_all x1 -> x0, blocking collectives: 27.4 us -> none  [from_everyone(): return lax.all_to_all(copies, axis, split_axis=0, concat_axis=0, tiled=True)]
    all_to_all x0 -> x2, starting transfers between devices: none -> 19.1 us  [the longest x1 14.5 us: from_everyone(): return lax.all_to_all(copies, axis, split_axis=0, concat_axis=0, tiled=True)]
    all_gather x1 -> x0, waiting for transfers between devices: 12.9 us -> none  [on_device(): ready_down = lax.all_gather(narrow_down, 'rows', axis=2, tiled=True)]
    another operation x0 -> x1, local copies, waits for them, and re-layouts: none -> 2.55 us  [on_device(): pieces = jnp.stack([narrow_down for _ in range(devices)])]
    unnamed x6 -> x5, local copies, waits for them, and re-layouts: 8.05 us -> 6.55 us
  transfers between devices with their start and end apart: 1 -> 2, of which waited for: 1 -> 2; matrix products, arithmetic and copies ran while one was open for 6% -> 2% of each run, Pallas kernels for 0% -> 0%
where the time goes in v1:
time: 161 us
  waiting for transfers between devices  107 us (66%)
  blocking collectives  19.4 us (12%)
  starting transfers between devices  19.1 us (12%)
  local copies, waits for them, and re-layouts  10.2 us (6%)
  other arithmetic  4.17 us (3%)
    all_to_all x1, waiting for transfers between devices, on_device(): pieces = lax.all_to_all(pieces, 'rows', split_axis=0, concat_axis=0)  95.7 us
    all_gather x1, blocking collectives, on_device(): row_router = lax.all_gather(part_router, 'rows', axis=0, tiled=True)  19.4 us
    all_to_all x1, starting transfers between devices, from_everyone(): return lax.all_to_all(copies, axis, split_axis=0, concat_axis=0, tiled=True)  14.5 us
    all_to_all x1, waiting for transfers between devices, from_everyone(): return lax.all_to_all(copies, axis, split_axis=0, concat_axis=0, tiled=True)  11.6 us
    unnamed x5, local copies, waits for them, and re-layouts  6.55 us
    all_to_all x1, starting transfers between devices, on_device(): pieces = lax.all_to_all(pieces, 'rows', split_axis=0, concat_axis=0)  4.55 us
  transfers between devices with their start and end apart: 2, of which 2 were waited for; matrix products, arithmetic and copies ran while one was open for 2% of the time, Pallas kernels for 0%

profile of v1, /device:TPU:1, one launch (start us, length us, event | category | flops | bytes accessed | tf_op | source)
XLA Modules:
  0.0 160.8 jit_solution(14133238966752416072)
XLA Ops:
  0.6 0.7 multiply_convert_fusion
  1.3 19.4 %all_gather.5 = bf16[2048,1]{0,1:T(2,128)(2,1)S(1)} all-gather(bf16[256,1]{0,1:T(2,128)(2,1)S(1)} %multiply_convert_fusion), channel_id=1, replica_groups=mesh['owner'=64,'rows'=8] {'rows'}, dimensions={0}, use_global_device_ids=true | all-gather | bytes 4608 | tf_op jit(solution)/shard_map/all_gather | solution.py:30
  20.8 0.3 broadcast_bitcast_fusion
  21.0 0.5 broadcast.5
  21.6 2.2 %reduce.1 = bf16[64,2048]{1,0:T(8,128)(2,1)S(1)} reduce(bf16[64,1,2048]{2,1,0:T(2,128)(2,1)S(1)} %broadcast_bitcast_fusion, bf16[]{:T(256)} %broadcast.5), dimensions={1}, to_apply=%broadcast_bitcast_fusion.reduce_sub_computation | reduce | bytes 524290
  23.7 0.9 reshape.21
  24.6 14.5 %all-to-all-start.1 = ((bf16[64,2,1024]{2,1,0:T(2,128)(2,1)}), bf16[64,2,1024]{2,1,0:T(2,128)(2,1)S(1)}, u32[]{:S(2)}, u32[]{:S(2)}) async-start(bf16[64,2,1024]{2,1,0:T(2,128)(2,1)} %reshape.21), calls=%async_computation.1 | async-start | bytes 524288 | tf_op jit(solution)/shard_map/all_to_all | solution.py:15
  39.2 1.3 convert_bitcast_fusion
  40.4 0.2 copy.7
  40.6 11.6 %all-to-all-done.1 = bf16[64,2,1024]{2,1,0:T(2,128)(2,1)S(1)} async-done(((bf16[64,2,1024]{2,1,0:T(2,128)(2,1)}), bf16[64,2,1024]{2,1,0:T(2,128)(2,1)S(1)}, u32[]{:S(2)}, u32[]{:S(2)}) %all-to-all-start.1) | async-done | bytes 262176 | tf_op jit(solution)/shard_map/all_to_all | solution.py:15
  52.2 2.6 %stack.2 = bf16[8,1,1024,256]{2,3,1,0:T(8,128)(2,1)} broadcast(bf16[1024,256]{0,1:T(8,128)(2,1)S(1)} %copy.7), dimensions={2,3} | broadcast | bytes 4718592 | tf_op jit(solution)/shard_map/stack | solution.py:25
  54.8 4.5 %all-to-all-start = ((bf16[8,1,1024,256]{2,3,1,0:T(8,128)(2,1)}), bf16[8,1,1024,256]{2,3,1,0:T(8,128)(2,1)}, u32[]{:S(2)}, u32[]{:S(2)}) async-start(bf16[8,1,1024,256]{2,3,1,0:T(8,128)(2,1)} %stack.2), calls=%async_computation | async-start | bytes 8388608 | tf_op jit(solution)/shard_map/all_to_all | solution.py:26
  59.3 0.2 reshape.22
  59.6 0.9 copy.10
  60.4 95.7 %all-to-all-done = bf16[8,1,1024,256]{2,3,1,0:T(8,128)(2,1)} async-done(((bf16[8,1,1024,256]{2,3,1,0:T(8,128)(2,1)}), bf16[8,1,1024,256]{2,3,1,0:T(8,128)(2,1)}, u32[]{:S(2)}, u32[]{:S(2)}) %all-to-all-start) | async-done | bytes 4194336 | tf_op jit(solution)/shard_map/all_to_all | solution.py:26
  156.1 4.6 %copy.12 = bf16[1,2048,1024]{2,1,0:T(8,128)(2,1)} copy(bf16[1,2048,1024]{2,1,0:T(8,128)(2,1)} %bitcast.3) | data formatting | bytes 8388608
  (1 shorter events, 0.0 us)
Async XLA Ops:
  24.6 27.6 %all-to-all-start.1 = ((bf16[64,2,1024]{2,1,0:T(2,128)(2,1)}), bf16[64,2,1024]{2,1,0:T(2,128)(2,1)S(1)}, u32[]{:S(2)}, u32[]{:S(2)}) async-start(bf16[64,2,1024]{2,1,0:T(2,128)(2,1)} %reshape.21), calls=%async_computation.1 | async-start | bytes 524288 | tf_op jit(solution)/shard_map/all_to_all | solution.py:15
  54.8 101.4 %all-to-all-start = ((bf16[8,1,1024,256]{2,3,1,0:T(8,128)(2,1)}), bf16[8,1,1024,256]{2,3,1,0:T(8,128)(2,1)}, u32[]{:S(2)}, u32[]{:S(2)}) async-start(bf16[8,1,1024,256]{2,3,1,0:T(8,128)(2,1)} %stack.2), calls=%async_computation | async-start | bytes 8388608 | tf_op jit(solution)/shard_map/all_to_all | solution.py:26
